TPU v7x, 32 devices: a whole 2x2x4 slice. The times are simulated.
32 devices in a mesh: row: 8 (over z, y), col: 4 (over x, core).
Axes of the slice: x: 2, y: 2, z: 4, core: 2. Of those that a mesh axis runs over, the one named last changes fastest.
Arguments:
- tokens: bfloat16 [256, 7168], P(('row', 'col')), may hold values from -6 to 6
- gate_weights: bfloat16 [256, 4], P(('row', 'col')), may hold values from 0.099609375 to 1
- expert_ids: int32 [256, 4], P(('row', 'col')), may hold values from 0 to 7, all different within a row; in each aligned block of 32 rows (0 to 31, 32 to 63, ...) at most 24 rows name the same one
- w_in: bfloat16 [4, 7168, 2, 4096], P('col', None, None, 'row'), may hold values from -0.0625 to 0.0625
- w_out: bfloat16 [4, 4096, 7168], P('col', 'row'), may hold values from -0.125 to 0.125
Outputs:
- combined: bfloat16 [256, 7168], P(('row', 'col'))
Inputs may be any that keep to these rules, and one draw needn't show every extreme that they name: `expert_ids`: each token names 4 different experts; in every aligned block of 32 rows (one token group) no expert is named by more than 24 rows, a bound that some block reaches.
All inputs are finite; a program needn't handle non-finite values.
Results may differ from a plain program's by a relative error of at most 0.018.
Values may be sent and summed in bfloat16 or wider, within the bound.
No kernel may reach another device: no remote copies, remote signals or barrier semaphores. Data moves between devices by JAX's collectives and lax.ppermute only.
A program may use at most 128 MiB of HBM per device.

v0:
```python
import jax
import jax.numpy as jnp
from jax import lax
from jax.sharding import PartitionSpec as P

EXP_DEV = 2
CAP = 24


def on_device(tokens, gate_weights, expert_ids, w_in, w_out):
    width = tokens.shape[1]
    column_count = lax.axis_size("col")
    row_count = lax.axis_size("row")
    expert_count = EXP_DEV
    capacity = CAP
    piece_count = row_count // expert_count
    units = w_out.shape[1]
    local_experts = lax.axis_index("col") * expert_count + jnp.arange(expert_count, dtype=jnp.int32)
    packed = (tokens, gate_weights, expert_ids.astype(jnp.bfloat16))
    all_tokens, all_gates, all_routes = (
        lax.all_gather(packed[0], "col", axis=0, tiled=True),
        lax.all_gather(packed[1], "col", axis=0, tiled=True),
        lax.all_gather(packed[2], "col", axis=0, tiled=True),
    )
    route_numbers = all_routes.astype(jnp.int32)
    hits = route_numbers[None, :, :] == local_experts[:, None, None]
    weight = jnp.sum(jnp.where(hits, all_gates.astype(jnp.float32)[None, :, :], 0.0), axis=2)
    is_live = (weight > 0.0).astype(jnp.int32)
    slot_index = jnp.cumsum(is_live, axis=1) - is_live
    places = jnp.arange(capacity, dtype=jnp.int32)
    selector = (
        (is_live[:, None, :] > 0) & (slot_index[:, None, :] == places[None, :, None])
    ).astype(jnp.bfloat16)
    routed = jnp.einsum(
        "jsn,nd->jsd", selector, all_tokens, preferred_element_type=jnp.float32
    ).astype(jnp.bfloat16)
    w_gate_up = w_in[0].reshape(width, 2 * units)
    w_down = w_out[0]
    outgoing = jnp.repeat(routed, piece_count, axis=0)
    arrived = lax.all_to_all(outgoing, "row", split_axis=0, concat_axis=0, tiled=True)
    gate_up = jnp.dot(arrived, w_gate_up, preferred_element_type=jnp.float32)
    hidden = (jax.nn.silu(gate_up[..., :units]) * gate_up[..., units:]).astype(jnp.bfloat16)
    partial_value = jnp.einsum(
        "gsu,ud->gsd", hidden, w_down, preferred_element_type=jnp.float32
    ).astype(jnp.bfloat16)
    gathered = lax.all_to_all(partial_value, "row", split_axis=0, concat_axis=0, tiled=True)
    summed = jnp.sum(
        gathered.reshape(expert_count, piece_count, capacity, width), axis=1, dtype=jnp.float32
    )
    expert_out = summed.astype(jnp.bfloat16)
    all_experts = jnp.arange(column_count * expert_count, dtype=jnp.int32)
    matches = expert_ids[:, None, :] == all_experts[None, :, None]
    gate_table = jnp.sum(
        jnp.where(matches, gate_weights.astype(jnp.float32)[:, None, :], 0.0), axis=2
    )
    returning = jnp.einsum(
        "jsn,jsd->njd", selector, expert_out, preferred_element_type=jnp.float32
    ).astype(jnp.bfloat16)
    returned = lax.all_to_all(returning, "col", split_axis=0, concat_axis=1, tiled=True)
    combined = jnp.sum(gate_table[:, :, None] * returned.astype(jnp.float32), axis=1)
    return combined.astype(jnp.bfloat16)


def solution(mesh):
    return jax.shard_map(
        on_device,
        mesh=mesh,
        in_specs=(
            P(("row", "col"), None),
            P(("row", "col"), None),
            P(("row", "col"), None),
            P("col", None, None, "row"),
            P("col", "row", None),
        ),
        out_specs=P(("row", "col"), None),
        check_vma=False,
    )
```

profile of v0, /device:TPU:0, one launch (start us, length us, event | category | flops | bytes accessed | tf_op | source)
XLA Modules:
  0.0 190.0 jit_solution(9528152346293133747)
XLA Ops:
  0.0 0.7 convert_bitcast_fusion.1
  0.7 6.0 %all-gather = bf16[4,8,4]{1,2,0:T(4,128)(2,1)S(1)} all-gather(bf16[1,8,4]{1,2,0:T(4,128)(2,1)S(1)} %convert_bitcast_fusion.1), channel_id=1, replica_groups=mesh['row'=8,'col'=4] {'col'}, dimensions={0}, use_global_device_ids=true | all-gather | bytes 320 | tf_op jit(solution)/shard_map/all_gather | solution.py:23
  6.7 0.1 reshape.44
  6.8 5.6 %all-gather.1 = bf16[4,8,4]{1,2,0:T(4,128)(2,1)S(1)} all-gather(bf16[1,8,4]{1,2,0:T(4,128)(2,1)} %bitcast.33), channel_id=1, replica_groups=mesh['row'=8,'col'=4] {'col'}, dimensions={0}, use_global_device_ids=true | all-gather | bytes 320 | tf_op jit(solution)/shard_map/all_gather | solution.py:22
  12.4 0.1 reshape.45
  12.5 0.1 select_reduce_fusion.1
  12.6 0.2 reduce_window_sum.11
  12.8 7.2 %all_gather.11 = bf16[32,7168]{1,0:T(8,128)(2,1)S(1)} all-gather(bf16[8,7168]{1,0:T(8,128)(2,1)} %param.5), channel_id=1, replica_groups=mesh['row'=8,'col'=4] {'col'}, dimensions={0}, use_global_device_ids=true | all-gather | bytes 573440 | tf_op jit(solution)/shard_map/all_gather | solution.py:21
  20.0 0.3 convolution_convert_fusion.2
  20.3 1.8 broadcast_in_dim.41
  22.1 5.9 %all-to-all-start = ((bf16[8,24,7168]{2,1,0:T(8,128)(2,1)}), bf16[8,24,7168]{2,1,0:T(8,128)(2,1)S(1)}, u32[]{:S(2)}, u32[]{:S(2)}) async-start(bf16[8,24,7168]{2,1,0:T(8,128)(2,1)} %bitcast.4), calls=%async_computation | async-start | bytes 5505024 | tf_op jit(solution)/shard_map/all_to_all | solution.py:40
  28.1 24.1 %reshape.47 = bf16[7168,1024,1]{1,0,2:T(8,128)(2,1)} reshape(bf16[1,7168,2,512]{3,2,1,0:T(2,128)(2,1)} %param.8) | data formatting | bytes 29360128 | tf_op jit(solution)/shard_map/reshape;squeeze | solution.py:37
  52.1 38.7 %all-to-all-done = bf16[8,24,7168]{2,1,0:T(8,128)(2,1)S(1)} async-done(((bf16[8,24,7168]{2,1,0:T(8,128)(2,1)}), bf16[8,24,7168]{2,1,0:T(8,128)(2,1)S(1)}, u32[]{:S(2)}, u32[]{:S(2)}) %all-to-all-start) | async-done | bytes 2752544 | tf_op jit(solution)/shard_map/all_to_all | solution.py:40
  90.9 6.8 %fusion.17 = f32[8,24,1024]{2,1,0:T(8,128)S(1)} fusion(bf16[8,24,7168]{2,1,0:T(8,128)(2,1)S(1)} %all-to-all-done, bf16[7168,1024,1]{1,0,2:T(8,128)(2,1)} %reshape.47), kind=kOutput, calls=%fused_computation.28 | convolution fusion | flops 2818572288 | bytes 18219008 | tf_op jit(solution)/shard_map/dot_general | solution.py:41
  97.7 4.7 %convolution_convert_fusion = bf16[8,24,7168]{2,1,0:T(8,128)(2,1)S(1)} fusion(bf16[1,512,7168]{2,1,0:T(8,128)(2,1)} %param.9, f32[8,24,1024]{2,1,0:T(8,128)S(1)} %fusion.17), kind=kOutput, calls=%fused_computation | convolution fusion | flops 1411252224 | bytes 10878976 | tf_op jit(solution)/shard_map/gsu,ud->gsd/dot_general | solution.py:43
  102.4 66.3 %all_to_all.19 = bf16[8,24,7168]{2,1,0:T(8,128)(2,1)S(1)} all-to-all(bf16[8,24,7168]{2,1,0:T(8,128)(2,1)S(1)} %convolution_convert_fusion), channel_id=1, replica_groups=mesh['row'=8,'col'=4] {'row'}, dimensions={0} | all-to-all | bytes 5505024 | tf_op jit(solution)/shard_map/all_to_all | solution.py:46
  168.7 0.4 bitcast_reduce_fusion
  169.1 0.0 copy-start.1
  169.1 0.0 copy-start
  169.1 0.4 fusion
  169.6 1.9 copy.25
  171.4 3.5 %all-to-all-start.2 = ((bf16[32,2,7168]{2,1,0:T(2,128)(2,1)}), bf16[32,2,7168]{2,1,0:T(2,128)(2,1)S(1)}, u32[]{:S(2)}, u32[]{:S(2)}) async-start(bf16[32,2,7168]{2,1,0:T(2,128)(2,1)} %copy.25), calls=%async_computation.2 | async-start | bytes 1835008 | tf_op jit(solution)/shard_map/all_to_all | solution.py:59
  175.0 0.0 copy-done.1
  175.0 0.0 copy-done
  175.0 0.1 select_reduce_fusion
  175.1 0.1 copy.21
  175.1 0.1 copy.22
  175.2 12.7 %all-to-all-done.2 = bf16[32,2,7168]{2,1,0:T(2,128)(2,1)S(1)} async-done(((bf16[32,2,7168]{2,1,0:T(2,128)(2,1)}), bf16[32,2,7168]{2,1,0:T(2,128)(2,1)S(1)}, u32[]{:S(2)}, u32[]{:S(2)}) %all-to-all-start.2) | async-done | bytes 917536 | tf_op jit(solution)/shard_map/all_to_all | solution.py:59
  188.0 2.1 %fusion.3 = bf16[8,7168]{1,0:T(8,128)(2,1)} fusion(bf16[4,8,2,7168]{3,2,1,0:T(2,128)(2,1)S(1)} %bitcast.31, f32[8,4,2]{2,0,1:T(8,128)S(1)} %copy.22), kind=kLoop, calls=%fused_computation.8 | loop fusion | flops 1318912 | bytes 1032448 | tf_op jit(solution)/shard_map/reduce_sum | solution.py:60
  (7 shorter events, 0.0 us)
Async XLA Ops:
  22.1 68.7 %all-to-all-start = ((bf16[8,24,7168]{2,1,0:T(8,128)(2,1)}), bf16[8,24,7168]{2,1,0:T(8,128)(2,1)S(1)}, u32[]{:S(2)}, u32[]{:S(2)}) async-start(bf16[8,24,7168]{2,1,0:T(8,128)(2,1)} %bitcast.4), calls=%async_computation | async-start | bytes 5505024 | tf_op jit(solution)/shard_map/all_to_all | solution.py:40
  169.1 5.9 %copy-start.1 = (bf16[8,4]{0,1:T(4,128)(2,1)S(1)}, bf16[8,4]{0,1:T(4,128)(2,1)}, u32[]{:S(2)}) copy-start(bf16[8,4]{0,1:T(4,128)(2,1)} %param.6) | copy-start | bytes 196
  169.1 5.9 %copy-start = (s32[8,4]{0,1:T(4,128)S(1)}, s32[8,4]{0,1:T(4,128)}, u32[]{:S(2)}) copy-start(s32[8,4]{0,1:T(4,128)} %param.7) | copy-start | bytes 388
  171.4 16.5 %all-to-all-start.2 = ((bf16[32,2,7168]{2,1,0:T(2,128)(2,1)}), bf16[32,2,7168]{2,1,0:T(2,128)(2,1)S(1)}, u32[]{:S(2)}, u32[]{:S(2)}) async-start(bf16[32,2,7168]{2,1,0:T(2,128)(2,1)} %copy.25), calls=%async_computation.2 | async-start | bytes 1835008 | tf_op jit(solution)/shard_map/all_to_all | solution.py:59
where the time goes:
time: 191 us; the launch traced here: 190 us
  blocking collectives  85.1 us (45%)
  waiting for transfers between devices  51.4 us (27%)
  local copies, waits for them, and re-layouts  28.1 us (15%)
  matrix products  12.3 us (6%)
  starting transfers between devices  9.44 us (5%)
  other arithmetic  3.58 us (2%)
    all_to_all x1, blocking collectives, on_device(): lax.all_to_all(partial_value, 'row', split_axis=0, concat_axis=0, tiled=T...  66.3 us
    all_to_all x1, waiting for transfers between devices, on_device(): lax.all_to_all(outgoing, 'row', split_axis=0, concat_axis=0, tiled=True)  38.7 us
    another operation x1, local copies, waits for them, and re-layouts, on_device(): w_gate_up = w_in[0].reshape(width, 2 * units)  24.1 us
    all_to_all x1, waiting for transfers between devices, on_device(): lax.all_to_all(returning, 'col', split_axis=0, concat_axis=1, tiled=True)  12.7 us
    all_gather x1, blocking collectives, on_device(): lax.all_gather(packed[0], 'col', axis=0, tiled=True)  7.22 us
    dot_general x1, matrix products, on_device(): gate_up = jnp.dot(arrived, w_gate_up, preferred_element_type=jnp.float32)  6.83 us
    all_gather x1, blocking collectives, on_device(): lax.all_gather(packed[2], 'col', axis=0, tiled=True)  6 us
    all_to_all x1, starting transfers between devices, on_device(): lax.all_to_all(outgoing, 'row', split_axis=0, concat_axis=0, tiled=True)  5.94 us
  transfers between devices with their start and end apart: 2, of which 2 were waited for; matrix products, arithmetic and copies ran while one was open for 13% of the time, Pallas kernels for 0%

commit v1 on v0

v1 whole, which is shorter than its diff:
```python
import jax
import jax.numpy as jnp
from jax import lax
from jax.sharding import PartitionSpec as P

EXP_DEV = 2
LANES = 128
AXES = ("row", "col")


def solution(mesh):
    rows, cols = mesh.shape["row"], mesh.shape["col"]
    sizes = {"z": rows // 2, "y": 2, "x": cols // 2, "c": 2}
    names = tuple(sizes)
    strides = {"c": 1, "x": 2, "y": cols, "z": 2 * cols}
    devices = rows * cols

    def swap(value, axis, distance):
        pairs = []
        for here in range(devices):
            place = here // strides[axis] % sizes[axis]
            pairs.append((here, here + ((place ^ distance) - place) * strides[axis]))
        return lax.ppermute(value, AXES, pairs)

    def gather(block, axis, at):
        got = {r: swap(block, axis, r) for r in reversed(range(1, sizes[axis]))}
        return jnp.stack([block] + [got[r] for r in range(1, sizes[axis])], axis=at)

    def scatter(value, axis, at):
        entry = lambda r: lax.index_in_dim(value, r, at, keepdims=False)
        got = [swap(entry(r), axis, r) for r in reversed(range(1, sizes[axis]))]
        total = entry(0).astype(jnp.float32)
        for part in got:
            total = total + part.astype(jnp.float32)
        return total.astype(jnp.bfloat16)

    def on_device(tokens, gate_weights, expert_ids, w_in, w_out):
        count, width = tokens.shape
        units = w_out.shape[1]
        experts = jnp.arange(LANES, dtype=jnp.int32)
        chosen = expert_ids[:, None, :] == experts[None, :, None]
        table = jnp.sum(jnp.where(chosen, gate_weights[:, None, :], 0), axis=2)
        packed = jnp.concatenate([tokens, table.astype(jnp.bfloat16)], axis=1)
        half = width // (2 * LANES) * LANES

        held = gather(packed, "z", 0)
        first, second = held[..., :half], held[..., half:]
        first = gather(gather(first, "x", 0), "y", 1)
        second = gather(gather(second, "y", 0), "x", 0)
        first = gather(first, "c", 0).reshape(-1, half)
        second = gather(second, "c", 0).reshape(-1, width + LANES - half)
        total = devices * count

        mine = lax.axis_index("col") * EXP_DEV + lax.axis_index("row") // (rows // EXP_DEV)
        gates = lax.dynamic_slice_in_dim(second, width - half + mine, 1, 1).astype(jnp.float32)
        everything = jnp.concatenate([first, second[:, : width - half]], axis=1)
        gate_up = jnp.dot(
            everything, w_in[0].reshape(width, 2 * units), preferred_element_type=jnp.float32
        )
        hidden = jax.nn.silu(gate_up[:, :units]) * gate_up[:, units:]
        hidden = hidden.astype(jnp.bfloat16)
        partial = jnp.dot(hidden, w_out[0], preferred_element_type=jnp.float32)
        partial = (partial * gates).astype(jnp.bfloat16)

        partial = partial.reshape(2, sizes["x"], 2, sizes["z"], count, width)
        partial = scatter(partial, "c", 0)
        first, second = partial[..., :half], partial[..., half:]
        first = scatter(scatter(first, "x", 0), "y", 0)
        second = scatter(scatter(second, "y", 1), "x", 0)
        return jnp.concatenate([scatter(first, "z", 0), scatter(second, "z", 0)], axis=1)

    return jax.shard_map(
        on_device,
        mesh=mesh,
        in_specs=(
            P(AXES, None),
            P(AXES, None),
            P(AXES, None),
            P("col", None, None, "row"),
            P("col", "row", None),
        ),
        out_specs=P(AXES, None),
        check_vma=False,
    )
```

time: 191 us -> 106 us (0.55)
  blocking collectives: 85.1 us -> 0 us
  starting transfers between devices: 9.44 us -> 28.4 us
  local copies, waits for them, and re-layouts: 28.1 us -> 16.3 us
  waiting for transfers between devices: 51.4 us -> 43.7 us
  other arithmetic: 3.58 us -> 7.51 us
  matrix products: 12.3 us -> 9.6 us
    all_to_all x1 -> x0, blocking collectives: 66.3 us -> none  [on_device(): lax.all_to_all(partial_value, 'row', split_axis=0, concat_axis=0, tiled=T...]
    all_to_all x2 -> x0, waiting for transfers between devices: 51.4 us -> none  [the longest x1 38.7 us: on_device(): lax.all_to_all(outgoing, 'row', split_axis=0, concat_axis=0, tiled=True)]
    ppermute x0 -> x20, waiting for transfers between devices: none -> 43.7 us  [swap(): return lax.ppermute(value, AXES, pairs)]
    ppermute x0 -> x20, starting transfers between devices: none -> 28.4 us  [swap(): return lax.ppermute(value, AXES, pairs)]
    another operation x1 -> x0, local copies, waits for them, and re-layouts: 24.1 us -> none  [on_device(): w_gate_up = w_in[0].reshape(width, 2 * units)]
    all_gather x3 -> x0, blocking collectives: 18.8 us -> none  [the longest x1 7.22 us: on_device(): lax.all_gather(packed[0], 'col', axis=0, tiled=True)]
    unnamed x4 -> x5, local copies, waits for them, and re-layouts: 0.01 us -> 15.7 us
    all_to_all x2 -> x0, starting transfers between devices: 9.44 us -> none  [the longest x1 5.94 us: on_device(): lax.all_to_all(outgoing, 'row', split_axis=0, concat_axis=0, tiled=True)]
  transfers between devices with their start and end apart: 2 -> 20, of which waited for: 2 -> 13; matrix products, arithmetic and copies ran while one was open for 13% -> 18% of each run, Pallas kernels for 0% -> 0%
where the time goes in v1:
time: 106 us
  waiting for transfers between devices  43.7 us (41%)
  starting transfers between devices  28.4 us (27%)
  local copies, waits for them, and re-layouts  16.3 us (15%)
  matrix products  9.6 us (9%)
  other arithmetic  7.51 us (7%)
    ppermute x20, waiting for transfers between devices, swap(): return lax.ppermute(value, AXES, pairs)  43.7 us
    ppermute x20, starting transfers between devices, swap(): return lax.ppermute(value, AXES, pairs)  28.4 us
    unnamed x5, local copies, waits for them, and re-layouts  15.7 us
    dot_general x1, matrix products, on_device(): jnp.dot(everything, w_in[0].reshape(width, 2 * units), preferred_element_...  7.42 us
    another operation x10, other arithmetic, gather(): return jnp.stack([block] + [got[r] for r in range(1, sizes[axis])], axis=at)  5.01 us
    dot_general x1, matrix products, on_device(): partial = jnp.dot(hidden, w_out[0], preferred_element_type=jnp.float32)  2.19 us
  transfers between devices with their start and end apart: 20, of which 13 were waited for; matrix products, arithmetic and copies ran while one was open for 18% of the time, Pallas kernels for 0%

profile of v1, /device:TPU:0, one launch (start us, length us, event | category | flops | bytes accessed | tf_op | source)
XLA Modules:
  0.0 105.7 jit_solution(15824549394853088281)
XLA Ops:
  0.0 0.8 fusion.21
  0.8 0.9 fusion.24
  1.7 4.1 %collective-permute-start.1 = (bf16[8,7296]{1,0:T(8,128)(2,1)S(1)}, bf16[8,7296]{1,0:T(8,128)(2,1)S(1)}, u32[]{:S(2)}, u32[]{:S(2)}) collective-permute-start(bf16[8,7296]{1,0:T(8,128)(2,1)S(1)} %get-tuple-element.24), channel_id=1, source_target_pairs={{0,16},{1,17},{2,18},{3,19},{4,20},{5,21},{6,22},{7,23},{8,24},{9,... | collective-permute-start | bytes 350216 | tf_op jit(solution)/shard_map/ppermute | solution.py:23
  5.8 1.6 %collective-permute-start = (bf16[8,7296]{1,0:T(8,128)(2,1)S(1)}, bf16[8,7296]{1,0:T(8,128)(2,1)S(1)}, u32[]{:S(2)}, u32[]{:S(2)}) collective-permute-start(bf16[8,7296]{1,0:T(8,128)(2,1)S(1)} %get-tuple-element.24), channel_id=1, source_target_pairs={{0,8},{1,9},{2,10},{3,11},{4,12},{5,13},{6,14},{7,15},{8,0},{9,1},... | collective-permute-start | bytes 350216 | tf_op jit(solution)/shard_map/ppermute | solution.py:23
  7.4 0.0 collective-permute-start.2
  7.4 5.8 %collective-permute-done.1 = bf16[8,7296]{1,0:T(8,128)(2,1)S(1)} collective-permute-done((bf16[8,7296]{1,0:T(8,128)(2,1)S(1)}, bf16[8,7296]{1,0:T(8,128)(2,1)S(1)}, u32[]{:S(2)}, u32[]{:S(2)}) %collective-permute-start.1) | collective-permute-done | bytes 116768 | tf_op jit(solution)/shard_map/ppermute | solution.py:23
  13.2 0.0 collective-permute-done
  13.2 1.9 %collective-permute-done.2 = bf16[8,7296]{1,0:T(8,128)(2,1)S(1)} collective-permute-done((bf16[8,7296]{1,0:T(8,128)(2,1)S(1)}, bf16[8,7296]{1,0:T(8,128)(2,1)S(1)}, u32[]{:S(2)}, u32[]{:S(2)}) %collective-permute-start.2) | collective-permute-done | bytes 116768 | tf_op jit(solution)/shard_map/ppermute | solution.py:23
  15.2 1.6 %collective-permute-start.3 = (bf16[4,8,3584]{2,1,0:T(8,128)(2,1)S(1)}, bf16[4,8,3584]{2,1,0:T(8,128)(2,1)S(1)}, u32[]{:S(2)}, u32[]{:S(2)}) collective-permute-start(bf16[4,8,3584]{2,1,0:T(8,128)(2,1)S(1)} %pad_maximum_fusion.9), channel_id=1, source_target_pairs={{0,2},{1,3},{2,0},{3,1},{4,6},{5,7},{6,4},{7,5},{8,10},{9,11},{10,... | collective-permute-start | bytes 688136 | tf_op jit(solution)/shard_map/ppermute | solution.py:23
  16.8 1.5 %collective-permute-start.6 = (bf16[4,8,3712]{2,1,0:T(8,128)(2,1)S(1)}, bf16[4,8,3712]{2,1,0:T(8,128)(2,1)S(1)}, u32[]{:S(2)}, u32[]{:S(2)}) collective-permute-start(bf16[4,8,3712]{2,1,0:T(8,128)(2,1)S(1)} %pad_maximum_fusion.6), channel_id=1, source_target_pairs={{0,4},{1,5},{2,6},{3,7},{4,0},{5,1},{6,2},{7,3},{8,12},{9,13},{10,... | collective-permute-start | bytes 712712 | tf_op jit(solution)/shard_map/ppermute | solution.py:23
  18.4 3.4 %collective-permute-done.3 = bf16[4,8,3584]{2,1,0:T(8,128)(2,1)S(1)} collective-permute-done((bf16[4,8,3584]{2,1,0:T(8,128)(2,1)S(1)}, bf16[4,8,3584]{2,1,0:T(8,128)(2,1)S(1)}, u32[]{:S(2)}, u32[]{:S(2)}) %collective-permute-start.3) | collective-permute-done | bytes 229408 | tf_op jit(solution)/shard_map/ppermute | solution.py:23
  21.8 0.1 fusion.25
  21.9 1.6 %collective-permute-start.4 = (bf16[2,4,8,3584]{3,2,1,0:T(8,128)(2,1)S(1)}, bf16[2,4,8,3584]{3,2,1,0:T(8,128)(2,1)S(1)}, u32[]{:S(2)}, u32[]{:S(2)}) collective-permute-start(bf16[2,4,8,3584]{3,2,1,0:T(8,128)(2,1)S(1)} %get-tuple-element.16), channel_id=1, source_target_pairs={{0,4},{1,5},{2,6},{3,7},{4,0},{5,1},{6,2},{7,3},{8,12},{9,13},{10,... | collective-permute-start | bytes 1376264 | tf_op jit(solution)/shard_map/ppermute | solution.py:23
  23.4 0.2 collective-permute-done.6
  23.7 0.1 fusion.26
  23.8 1.3 %collective-permute-start.7 = (bf16[2,4,8,3712]{3,2,1,0:T(8,128)(2,1)S(1)}, bf16[2,4,8,3712]{3,2,1,0:T(8,128)(2,1)S(1)}, u32[]{:S(2)}, u32[]{:S(2)}) collective-permute-start(bf16[2,4,8,3712]{3,2,1,0:T(8,128)(2,1)S(1)} %get-tuple-element.14), channel_id=1, source_target_pairs={{0,2},{1,3},{2,0},{3,1},{4,6},{5,7},{6,4},{7,5},{8,10},{9,11},{10,... | collective-permute-start | bytes 1425416 | tf_op jit(solution)/shard_map/ppermute | solution.py:23
  25.1 7.9 %collective-permute-done.4 = bf16[2,4,8,3584]{3,2,1,0:T(8,128)(2,1)S(1)} collective-permute-done((bf16[2,4,8,3584]{3,2,1,0:T(8,128)(2,1)S(1)}, bf16[2,4,8,3584]{3,2,1,0:T(8,128)(2,1)S(1)}, u32[]{:S(2)}, u32[]{:S(2)}) %collective-permute-start.4) | collective-permute-done | bytes 458784 | tf_op jit(solution)/shard_map/ppermute | solution.py:23
  33.0 1.1 fusion.27
  34.1 0.0 collective-permute-start.5
  34.1 0.1 collective-permute-done.7
  34.2 0.1 fusion.28
  34.3 0.5 collective-permute-start.8
  34.8 15.7 %copy.22 = bf16[896,8,2,512]{3,1,2,0:T(8,128)(2,1)} copy(bf16[896,8,2,512]{3,2,1,0:T(2,128)(2,1)} %bitcast.89) | data formatting | bytes 29360128
  50.5 0.0 collective-permute-done.5
  50.5 1.3 %pad_maximum_fusion.1 = bf16[2,2,2,4,8,3584]{5,4,3,2,1,0:T(8,128)(2,1)S(1)} fusion(bf16[1,2,2,4,8,3584]{5,4,3,2,1,0:T(8,128)(2,1)} %bitcast.10, bf16[1,2,2,4,8,3584]{5,4,3,2,1,0:T(8,128)(2,1)S(1)} %get-tuple-element.11), kind=kLoop, calls=%fused_computation.10 | loop fusion | flops 917504 | bytes 3670016 | tf_op jit(solution)/shard_map/stack | solution.py:27
  51.8 0.0 collective-permute-done.8
  51.8 1.4 %pad_maximum_fusion = bf16[2,2,2,4,8,3712]{5,4,3,2,1,0:T(8,128)(2,1)S(1)} fusion(bf16[1,2,2,4,8,3712]{5,4,3,2,1,0:T(8,128)(2,1)} %bitcast.17, bf16[1,2,2,4,8,3712]{5,4,3,2,1,0:T(8,128)(2,1)S(1)} %get-tuple-element.9), kind=kLoop, calls=%fused_computation.9 | loop fusion | flops 950272 | bytes 3801088 | tf_op jit(solution)/shard_map/stack | solution.py:27
  53.2 0.0 slice-start
  53.2 0.1 slice.100
  53.4 0.2 convert_reduce_fusion
  53.5 0.0 slice-start.1
  53.6 7.4 %fusion.2 = f32[256,1024]{1,0:T(8,128)S(1)} fusion(bf16[7168,1024]{1,0:T(8,128)(2,1)} %bitcast.90, bf16[256,3584]{1,0:T(8,128)(2,1)S(1)} %slice.100, bf16[256,3584]{1,0:T(8,128)(2,1)S(1)} %bitcast.107), kind=kOutput, calls=%fused_computation.3 | convolution fusion | flops 3765436416 | bytes 19398656 | tf_op jit(solution)/shard_map/dot_general | solution.py:57
  61.0 0.0 slice-done
  61.0 0.0 slice-done.1
  61.0 2.2 %fusion = bf16[256,7168]{1,0:T(8,128)(2,1)S(1)} fusion(bf16[1,512,7168]{2,1,0:T(8,128)(2,1)S(1)} %bitcast.113, f32[256]{0:T(256)S(1)} %convert_reduce_fusion, f32[256,1024]{1,0:T(8,128)S(1)} %fusion.2), kind=kOutput, calls=%fused_computation.1 | convolution fusion | flops 1883504640 | bytes 12059648 | tf_op jit(solution)/shard_map/dot_general | solution.py:62
  63.2 0.2 fusion.29
  63.5 0.1 copy.18
  63.6 0.2 collective-permute-start.9
  63.8 3.7 %collective-permute-done.9 = bf16[2,2,4,8,7168]{4,3,2,0,1:T(8,128)(2,1)S(1)} collective-permute-done((bf16[2,2,4,8,7168]{4,3,2,0,1:T(8,128)(2,1)S(1)}, bf16[2,2,4,8,7168]{4,3,2,0,1:T(8,128)(2,1)S(1)}, u32[]{:S(2)}, u32[]{:S(2)}) %collective-permute-start.9) | collective-permute-done | bytes 1835040 | tf_op jit(solution)/shard_map/ppermute | solution.py:23
  67.4 0.4 fusion.6
  68.0 1.3 %collective-permute-start.10 = (bf16[2,4,8,3584]{3,2,1,0:T(8,128)(2,1)S(1)}, bf16[2,4,8,3584]{3,2,1,0:T(8,128)(2,1)S(1)}, u32[]{:S(2)}, u32[]{:S(2)}) collective-permute-start(bf16[2,4,8,3584]{3,2,1,0:T(8,128)(2,1)S(1)} %slice_bitcast_fusion.2), channel_id=1, source_target_pairs={{0,2},{1,3},{2,0},{3,1},{4,6},{5,7},{6,4},{7,5},{8,10},{9,11},{10,... | collective-permute-start | bytes 1376264 | tf_op jit(solution)/shard_map/ppermute | solution.py:23
  69.3 1.2 %collective-permute-start.15 = (bf16[2,4,8,3584]{3,2,1,0:T(8,128)(2,1)S(1)}, bf16[2,4,8,3584]{3,2,1,0:T(8,128)(2,1)S(1)}, u32[]{:S(2)}, u32[]{:S(2)}) collective-permute-start(bf16[2,4,8,3584]{3,2,1,0:T(8,128)(2,1)S(1)} %slice_bitcast_fusion), channel_id=1, source_target_pairs={{0,4},{1,5},{2,6},{3,7},{4,0},{5,1},{6,2},{7,3},{8,12},{9,13},{10,... | collective-permute-start | bytes 1376264 | tf_op jit(solution)/shard_map/ppermute | solution.py:23
  70.5 10.1 %collective-permute-done.10 = bf16[2,4,8,3584]{3,2,1,0:T(8,128)(2,1)S(1)} collective-permute-done((bf16[2,4,8,3584]{3,2,1,0:T(8,128)(2,1)S(1)}, bf16[2,4,8,3584]{3,2,1,0:T(8,128)(2,1)S(1)}, u32[]{:S(2)}, u32[]{:S(2)}) %collective-permute-start.10) | collective-permute-done | bytes 458784 | tf_op jit(solution)/shard_map/ppermute | solution.py:23
  80.6 1.2 %collective-permute-done.15 = bf16[2,4,8,3584]{3,2,1,0:T(8,128)(2,1)S(1)} collective-permute-done((bf16[2,4,8,3584]{3,2,1,0:T(8,128)(2,1)S(1)}, bf16[2,4,8,3584]{3,2,1,0:T(8,128)(2,1)S(1)}, u32[]{:S(2)}, u32[]{:S(2)}) %collective-permute-start.15) | collective-permute-done | bytes 458784 | tf_op jit(solution)/shard_map/ppermute | solution.py:23
  81.8 0.3 fusion.8
  82.1 0.6 collective-permute-start.16
  82.7 1.6 %collective-permute-start.11 = (bf16[4,8,3584]{2,1,0:T(8,128)(2,1)S(1)}, bf16[4,8,3584]{2,1,0:T(8,128)(2,1)S(1)}, u32[]{:S(2)}, u32[]{:S(2)}) collective-permute-start(bf16[4,8,3584]{2,1,0:T(8,128)(2,1)S(1)} %slice_bitcast_fusion.6), channel_id=1, source_target_pairs={{0,4},{1,5},{2,6},{3,7},{4,0},{5,1},{6,2},{7,3},{8,12},{9,13},{10,... | collective-permute-start | bytes 688136 | tf_op jit(solution)/shard_map/ppermute | solution.py:23
  84.3 4.6 %collective-permute-done.16 = bf16[4,8,3584]{2,1,0:T(8,128)(2,1)S(1)} collective-permute-done((bf16[4,8,3584]{2,1,0:T(8,128)(2,1)S(1)}, bf16[4,8,3584]{2,1,0:T(8,128)(2,1)S(1)}, u32[]{:S(2)}, u32[]{:S(2)}) %collective-permute-start.16) | collective-permute-done | bytes 229408 | tf_op jit(solution)/shard_map/ppermute | solution.py:23
  88.9 0.1 fusion.10
  89.0 2.4 %collective-permute-start.17 = (bf16[8,3584]{1,0:T(8,128)(2,1)S(1)}, bf16[8,3584]{1,0:T(8,128)(2,1)S(1)}, u32[]{:S(2)}, u32[]{:S(2)}) collective-permute-start(bf16[8,3584]{1,0:T(8,128)(2,1)S(1)} %get-tuple-element.20), channel_id=1, source_target_pairs={{0,24},{1,25},{2,26},{3,27},{4,28},{5,29},{6,30},{7,31},{8,16},{9,... | collective-permute-start | bytes 172040 | tf_op jit(solution)/shard_map/ppermute | solution.py:23
  91.3 4.3 %collective-permute-start.19 = (bf16[8,3584]{1,0:T(8,128)(2,1)S(1)}, bf16[8,3584]{1,0:T(8,128)(2,1)S(1)}, u32[]{:S(2)}, u32[]{:S(2)}) collective-permute-start(bf16[8,3584]{1,0:T(8,128)(2,1)S(1)} %get-tuple-element.21), channel_id=1, source_target_pairs={{0,8},{1,9},{2,10},{3,11},{4,12},{5,13},{6,14},{7,15},{8,0},{9,1},... | collective-permute-start | bytes 172040 | tf_op jit(solution)/shard_map/ppermute | solution.py:23
  95.7 0.0 collective-permute-start.18
  95.7 0.0 collective-permute-done.11
  95.7 0.1 fusion.11
  95.7 2.4 %collective-permute-start.12 = (bf16[8,3584]{1,0:T(8,128)(2,1)S(1)}, bf16[8,3584]{1,0:T(8,128)(2,1)S(1)}, u32[]{:S(2)}, u32[]{:S(2)}) collective-permute-start(bf16[8,3584]{1,0:T(8,128)(2,1)S(1)} %get-tuple-element.17), channel_id=1, source_target_pairs={{0,24},{1,25},{2,26},{3,27},{4,28},{5,29},{6,30},{7,31},{8,16},{9,... | collective-permute-start | bytes 172040 | tf_op jit(solution)/shard_map/ppermute | solution.py:23
  98.2 1.1 %collective-permute-start.14 = (bf16[8,3584]{1,0:T(8,128)(2,1)S(1)}, bf16[8,3584]{1,0:T(8,128)(2,1)S(1)}, u32[]{:S(2)}, u32[]{:S(2)}) collective-permute-start(bf16[8,3584]{1,0:T(8,128)(2,1)S(1)} %get-tuple-element.18), channel_id=1, source_target_pairs={{0,8},{1,9},{2,10},{3,11},{4,12},{5,13},{6,14},{7,15},{8,0},{9,1},... | collective-permute-start | bytes 172040 | tf_op jit(solution)/shard_map/ppermute | solution.py:23
  99.3 0.0 collective-permute-done.17
  99.3 1.0 collective-permute-start.13
  100.3 0.0 collective-permute-done.19
  100.3 2.6 %collective-permute-done.18 = bf16[8,3584]{1,0:T(8,128)(2,1)S(1)} collective-permute-done((bf16[8,3584]{1,0:T(8,128)(2,1)S(1)}, bf16[8,3584]{1,0:T(8,128)(2,1)S(1)}, u32[]{:S(2)}, u32[]{:S(2)}) %collective-permute-start.18) | collective-permute-done | bytes 57376 | tf_op jit(solution)/shard_map/ppermute | solution.py:23
  102.9 0.0 collective-permute-done.12
  102.9 0.5 collective-permute-done.14
  103.4 1.6 %collective-permute-done.13 = bf16[8,3584]{1,0:T(8,128)(2,1)S(1)} collective-permute-done((bf16[8,3584]{1,0:T(8,128)(2,1)S(1)}, bf16[8,3584]{1,0:T(8,128)(2,1)S(1)}, u32[]{:S(2)}, u32[]{:S(2)}) %collective-permute-start.13) | collective-permute-done | bytes 57376 | tf_op jit(solution)/shard_map/ppermute | solution.py:23
  105.0 0.7 pad_maximum_fusion.11
  (13 shorter events, 0.3 us)
Async XLA Ops:
  1.7 11.5 %collective-permute-start.1 = (bf16[8,7296]{1,0:T(8,128)(2,1)S(1)}, bf16[8,7296]{1,0:T(8,128)(2,1)S(1)}, u32[]{:S(2)}, u32[]{:S(2)}) collective-permute-start(bf16[8,7296]{1,0:T(8,128)(2,1)S(1)} %get-tuple-element.24), channel_id=1, source_target_pairs={{0,16},{1,17},{2,18},{3,19},{4,20},{5,21},{6,22},{7,23},{8,24},{9,... | collective-permute-start | bytes 350216 | tf_op jit(solution)/shard_map/ppermute | solution.py:23
  5.8 7.4 %collective-permute-start = (bf16[8,7296]{1,0:T(8,128)(2,1)S(1)}, bf16[8,7296]{1,0:T(8,128)(2,1)S(1)}, u32[]{:S(2)}, u32[]{:S(2)}) collective-permute-start(bf16[8,7296]{1,0:T(8,128)(2,1)S(1)} %get-tuple-element.24), channel_id=1, source_target_pairs={{0,8},{1,9},{2,10},{3,11},{4,12},{5,13},{6,14},{7,15},{8,0},{9,1},... | collective-permute-start | bytes 350216 | tf_op jit(solution)/shard_map/ppermute | solution.py:23
  7.4 7.7 %collective-permute-start.2 = (bf16[8,7296]{1,0:T(8,128)(2,1)S(1)}, bf16[8,7296]{1,0:T(8,128)(2,1)S(1)}, u32[]{:S(2)}, u32[]{:S(2)}) collective-permute-start(bf16[8,7296]{1,0:T(8,128)(2,1)S(1)} %get-tuple-element.24), channel_id=1, source_target_pairs={{0,24},{1,25},{2,26},{3,27},{4,28},{5,29},{6,30},{7,31},{8,16},{9,... | collective-permute-start | bytes 350216 | tf_op jit(solution)/shard_map/ppermute | solution.py:23
  15.2 6.6 %collective-permute-start.3 = (bf16[4,8,3584]{2,1,0:T(8,128)(2,1)S(1)}, bf16[4,8,3584]{2,1,0:T(8,128)(2,1)S(1)}, u32[]{:S(2)}, u32[]{:S(2)}) collective-permute-start(bf16[4,8,3584]{2,1,0:T(8,128)(2,1)S(1)} %pad_maximum_fusion.9), channel_id=1, source_target_pairs={{0,2},{1,3},{2,0},{3,1},{4,6},{5,7},{6,4},{7,5},{8,10},{9,11},{10,... | collective-permute-start | bytes 688136 | tf_op jit(solution)/shard_map/ppermute | solution.py:23
  16.8 6.9 %collective-permute-start.6 = (bf16[4,8,3712]{2,1,0:T(8,128)(2,1)S(1)}, bf16[4,8,3712]{2,1,0:T(8,128)(2,1)S(1)}, u32[]{:S(2)}, u32[]{:S(2)}) collective-permute-start(bf16[4,8,3712]{2,1,0:T(8,128)(2,1)S(1)} %pad_maximum_fusion.6), channel_id=1, source_target_pairs={{0,4},{1,5},{2,6},{3,7},{4,0},{5,1},{6,2},{7,3},{8,12},{9,13},{10,... | collective-permute-start | bytes 712712 | tf_op jit(solution)/shard_map/ppermute | solution.py:23
  21.9 11.2 %collective-permute-start.4 = (bf16[2,4,8,3584]{3,2,1,0:T(8,128)(2,1)S(1)}, bf16[2,4,8,3584]{3,2,1,0:T(8,128)(2,1)S(1)}, u32[]{:S(2)}, u32[]{:S(2)}) collective-permute-start(bf16[2,4,8,3584]{3,2,1,0:T(8,128)(2,1)S(1)} %get-tuple-element.16), channel_id=1, source_target_pairs={{0,4},{1,5},{2,6},{3,7},{4,0},{5,1},{6,2},{7,3},{8,12},{9,13},{10,... | collective-permute-start | bytes 1376264 | tf_op jit(solution)/shard_map/ppermute | solution.py:23
  23.8 10.4 %collective-permute-start.7 = (bf16[2,4,8,3712]{3,2,1,0:T(8,128)(2,1)S(1)}, bf16[2,4,8,3712]{3,2,1,0:T(8,128)(2,1)S(1)}, u32[]{:S(2)}, u32[]{:S(2)}) collective-permute-start(bf16[2,4,8,3712]{3,2,1,0:T(8,128)(2,1)S(1)} %get-tuple-element.14), channel_id=1, source_target_pairs={{0,2},{1,3},{2,0},{3,1},{4,6},{5,7},{6,4},{7,5},{8,10},{9,11},{10,... | collective-permute-start | bytes 1425416 | tf_op jit(solution)/shard_map/ppermute | solution.py:23
  34.1 16.4 %collective-permute-start.5 = (bf16[2,2,4,8,3584]{4,3,2,1,0:T(8,128)(2,1)}, bf16[2,2,4,8,3584]{4,3,2,1,0:T(8,128)(2,1)}, u32[]{:S(2)}, u32[]{:S(2)}) collective-permute-start(bf16[2,2,4,8,3584]{4,3,2,1,0:T(8,128)(2,1)} %get-tuple-element.12), channel_id=1, source_target_pairs={{0,1},{1,0},{2,3},{3,2},{4,5},{5,4},{6,7},{7,6},{8,9},{9,8},{10,11... | collective-permute-start | bytes 2752520 | tf_op jit(solution)/shard_map/ppermute | solution.py:23
  34.3 17.5 %collective-permute-start.8 = (bf16[2,2,4,8,3712]{4,3,2,1,0:T(8,128)(2,1)S(1)}, bf16[2,2,4,8,3712]{4,3,2,1,0:T(8,128)(2,1)}, u32[]{:S(2)}, u32[]{:S(2)}) collective-permute-start(bf16[2,2,4,8,3712]{4,3,2,1,0:T(8,128)(2,1)S(1)} %get-tuple-element.10), channel_id=1, source_target_pairs={{0,1},{1,0},{2,3},{3,2},{4,5},{5,4},{6,7},{7,6},{8,9},{9,8},{10,11... | collective-permute-start | bytes 2850824 | tf_op jit(solution)/shard_map/ppermute | solution.py:23
  53.2 7.8 %slice-start = ((s8[7340032]{0:T(1024)(128)(4,1)}), s8[4194304]{0:T(1024)(128)(4,1)S(1)}, s32[]{:S(2)}) async-start(s8[7340032]{0:T(1024)(128)(4,1)} %bitcast.112), calls=%async_computation | async-start | bytes 8388608
  53.5 7.5 %slice-start.1 = ((s8[7340032]{0:T(1024)(128)(4,1)}), s8[3145728]{0:T(1024)(128)(4,1)S(1)}, s32[]{:S(2)}) async-start(s8[7340032]{0:T(1024)(128)(4,1)} %bitcast.112), calls=%async_computation.1 | async-start | bytes 6291456
  63.6 3.9 %collective-permute-start.9 = (bf16[2,2,4,8,7168]{4,3,2,0,1:T(8,128)(2,1)S(1)}, bf16[2,2,4,8,7168]{4,3,2,0,1:T(8,128)(2,1)S(1)}, u32[]{:S(2)}, u32[]{:S(2)}) collective-permute-start(bf16[2,2,4,8,7168]{4,3,2,0,1:T(8,128)(2,1)S(1)} %copy.18), channel_id=1, source_target_pairs={{0,1},{1,0},{2,3},{3,2},{4,5},{5,4},{6,7},{7,6},{8,9},{9,8},{10,11... | collective-permute-start | bytes 5505032 | tf_op jit(solution)/shard_map/ppermute | solution.py:23
  68.0 12.6 %collective-permute-start.10 = (bf16[2,4,8,3584]{3,2,1,0:T(8,128)(2,1)S(1)}, bf16[2,4,8,3584]{3,2,1,0:T(8,128)(2,1)S(1)}, u32[]{:S(2)}, u32[]{:S(2)}) collective-permute-start(bf16[2,4,8,3584]{3,2,1,0:T(8,128)(2,1)S(1)} %slice_bitcast_fusion.2), channel_id=1, source_target_pairs={{0,2},{1,3},{2,0},{3,1},{4,6},{5,7},{6,4},{7,5},{8,10},{9,11},{10,... | collective-permute-start | bytes 1376264 | tf_op jit(solution)/shard_map/ppermute | solution.py:23
  69.3 12.5 %collective-permute-start.15 = (bf16[2,4,8,3584]{3,2,1,0:T(8,128)(2,1)S(1)}, bf16[2,4,8,3584]{3,2,1,0:T(8,128)(2,1)S(1)}, u32[]{:S(2)}, u32[]{:S(2)}) collective-permute-start(bf16[2,4,8,3584]{3,2,1,0:T(8,128)(2,1)S(1)} %slice_bitcast_fusion), channel_id=1, source_target_pairs={{0,4},{1,5},{2,6},{3,7},{4,0},{5,1},{6,2},{7,3},{8,12},{9,13},{10,... | collective-permute-start | bytes 1376264 | tf_op jit(solution)/shard_map/ppermute | solution.py:23
  82.1 6.8 %collective-permute-start.16 = (bf16[4,8,3584]{2,1,0:T(8,128)(2,1)S(1)}, bf16[4,8,3584]{2,1,0:T(8,128)(2,1)S(1)}, u32[]{:S(2)}, u32[]{:S(2)}) collective-permute-start(bf16[4,8,3584]{2,1,0:T(8,128)(2,1)S(1)} %slice_bitcast_fusion.4), channel_id=1, source_target_pairs={{0,2},{1,3},{2,0},{3,1},{4,6},{5,7},{6,4},{7,5},{8,10},{9,11},{10,... | collective-permute-start | bytes 688136 | tf_op jit(solution)/shard_map/ppermute | solution.py:23
  82.7 13.0 %collective-permute-start.11 = (bf16[4,8,3584]{2,1,0:T(8,128)(2,1)S(1)}, bf16[4,8,3584]{2,1,0:T(8,128)(2,1)S(1)}, u32[]{:S(2)}, u32[]{:S(2)}) collective-permute-start(bf16[4,8,3584]{2,1,0:T(8,128)(2,1)S(1)} %slice_bitcast_fusion.6), channel_id=1, source_target_pairs={{0,4},{1,5},{2,6},{3,7},{4,0},{5,1},{6,2},{7,3},{8,12},{9,13},{10,... | collective-permute-start | bytes 688136 | tf_op jit(solution)/shard_map/ppermute | solution.py:23
  89.0 10.4 %collective-permute-start.17 = (bf16[8,3584]{1,0:T(8,128)(2,1)S(1)}, bf16[8,3584]{1,0:T(8,128)(2,1)S(1)}, u32[]{:S(2)}, u32[]{:S(2)}) collective-permute-start(bf16[8,3584]{1,0:T(8,128)(2,1)S(1)} %get-tuple-element.20), channel_id=1, source_target_pairs={{0,24},{1,25},{2,26},{3,27},{4,28},{5,29},{6,30},{7,31},{8,16},{9,... | collective-permute-start | bytes 172040 | tf_op jit(solution)/shard_map/ppermute | solution.py:23
  91.3 9.0 %collective-permute-start.19 = (bf16[8,3584]{1,0:T(8,128)(2,1)S(1)}, bf16[8,3584]{1,0:T(8,128)(2,1)S(1)}, u32[]{:S(2)}, u32[]{:S(2)}) collective-permute-start(bf16[8,3584]{1,0:T(8,128)(2,1)S(1)} %get-tuple-element.21), channel_id=1, source_target_pairs={{0,8},{1,9},{2,10},{3,11},{4,12},{5,13},{6,14},{7,15},{8,0},{9,1},... | collective-permute-start | bytes 172040 | tf_op jit(solution)/shard_map/ppermute | solution.py:23
  95.7 7.2 %collective-permute-start.18 = (bf16[8,3584]{1,0:T(8,128)(2,1)S(1)}, bf16[8,3584]{1,0:T(8,128)(2,1)S(1)}, u32[]{:S(2)}, u32[]{:S(2)}) collective-permute-start(bf16[8,3584]{1,0:T(8,128)(2,1)S(1)} %get-tuple-element.22), channel_id=1, source_target_pairs={{0,16},{1,17},{2,18},{3,19},{4,20},{5,21},{6,22},{7,23},{8,24},{9,... | collective-permute-start | bytes 172040 | tf_op jit(solution)/shard_map/ppermute | solution.py:23
  95.7 7.2 %collective-permute-start.12 = (bf16[8,3584]{1,0:T(8,128)(2,1)S(1)}, bf16[8,3584]{1,0:T(8,128)(2,1)S(1)}, u32[]{:S(2)}, u32[]{:S(2)}) collective-permute-start(bf16[8,3584]{1,0:T(8,128)(2,1)S(1)} %get-tuple-element.17), channel_id=1, source_target_pairs={{0,24},{1,25},{2,26},{3,27},{4,28},{5,29},{6,30},{7,31},{8,16},{9,... | collective-permute-start | bytes 172040 | tf_op jit(solution)/shard_map/ppermute | solution.py:23
  98.2 5.2 %collective-permute-start.14 = (bf16[8,3584]{1,0:T(8,128)(2,1)S(1)}, bf16[8,3584]{1,0:T(8,128)(2,1)S(1)}, u32[]{:S(2)}, u32[]{:S(2)}) collective-permute-start(bf16[8,3584]{1,0:T(8,128)(2,1)S(1)} %get-tuple-element.18), channel_id=1, source_target_pairs={{0,8},{1,9},{2,10},{3,11},{4,12},{5,13},{6,14},{7,15},{8,0},{9,1},... | collective-permute-start | bytes 172040 | tf_op jit(solution)/shard_map/ppermute | solution.py:23
  99.3 5.7 %collective-permute-start.13 = (bf16[8,3584]{1,0:T(8,128)(2,1)S(1)}, bf16[8,3584]{1,0:T(8,128)(2,1)S(1)}, u32[]{:S(2)}, u32[]{:S(2)}) collective-permute-start(bf16[8,3584]{1,0:T(8,128)(2,1)S(1)} %get-tuple-element.19), channel_id=1, source_target_pairs={{0,16},{1,17},{2,18},{3,19},{4,20},{5,21},{6,22},{7,23},{8,24},{9,... | collective-permute-start | bytes 172040 | tf_op jit(solution)/shard_map/ppermute | solution.py:23

commit v2 on v1

v2 whole, which is shorter than its diff:
```python
import functools

import jax
import jax.numpy as jnp
from jax import lax
from jax.experimental import pallas as pl
from jax.experimental.pallas import tpu as pltpu
from jax.sharding import PartitionSpec as P

EXP_DEV = 2
LANES = 128
AXES = ("row", "col")
RING = 4
IN_VMEM = pl.BlockSpec(memory_space=pltpu.VMEM)
IN_HBM = pl.BlockSpec(memory_space=pltpu.HBM)
IN_SMEM = pl.BlockSpec(memory_space=pltpu.SMEM)


def gate_up_kernel(pieces, step, units, first_step, last, *refs):
    token_refs, weights = refs[:pieces], refs[pieces]
    if last:
        before, mine, out = refs[pieces + 1 : pieces + 4]
    else:
        out = refs[pieces + 1]
    landing, arrived, even, odd, total = refs[-5:]
    per = 2 * units // LANES
    block = per * step
    steps = (token_refs[0].shape[1] - (LANES if last else 0)) // step
    wide = (even, odd)

    def fetch(k):
        return pltpu.make_async_copy(
            weights.at[pl.ds((first_step + k) * block, block), :],
            landing.at[k % RING],
            arrived.at[k % RING],
        )

    def unpack(k):
        fetch(k).wait()
        piece = min(block, 512)
        for at in range(0, block, piece):
            wide[k % 2][pl.ds(at, piece), :] = landing[k % RING, pl.ds(at, piece), :].astype(
                jnp.float32
            )
        if k + RING < steps:
            fetch(k + RING).start()

    for k in range(min(RING, steps)):
        fetch(k).start()
    total[...] = before[...] if last else jnp.zeros_like(total)
    unpack(0)
    for k in range(steps):
        if k + 1 < steps:
            unpack(k + 1)
        tokens = jnp.concatenate([ref[:, k * step : (k + 1) * step] for ref in token_refs], axis=0)
        for g in range(2):
            columns = [
                wide[k % 2][pl.ds(2 * f + g, step, stride=per), :].astype(jnp.bfloat16)
                for f in range(units // LANES)
            ]
            total[:, g * units : (g + 1) * units] += jnp.dot(
                tokens, jnp.concatenate(columns, axis=1), preferred_element_type=jnp.float32
            )
    if not last:
        out[...] = total[...]
        return
    table = jnp.concatenate([ref[:, -LANES:] for ref in token_refs], axis=0).astype(jnp.float32)
    lane = lax.broadcasted_iota(jnp.int32, table.shape, 1)
    gates = jnp.sum(jnp.where(lane == mine[0], table, 0.0), axis=1, keepdims=True)
    gate = total[:, :units]
    out[...] = (gate / (1 + jnp.exp(-gate)) * total[:, units:] * gates).astype(jnp.bfloat16)


def gate_up(pieces, weights, units, step, start, before=None, mine=None):
    last = before is not None
    rows = sum(piece.shape[0] for piece in pieces)
    depth = pieces[0].shape[1] - (LANES if last else 0)
    block = 2 * units // LANES * step
    shape = (rows, units if last else 2 * units)
    return pl.pallas_call(
        functools.partial(gate_up_kernel, len(pieces), step, units, start // step, last),
        out_shape=jax.ShapeDtypeStruct(shape, jnp.bfloat16 if last else jnp.float32),
        in_specs=[IN_VMEM] * len(pieces) + [IN_HBM] + ([IN_VMEM, IN_SMEM] if last else []),
        out_specs=IN_VMEM,
        scratch_shapes=[
            pltpu.VMEM((RING, block, LANES), jnp.bfloat16),
            pltpu.SemaphoreType.DMA((RING,)),
            pltpu.VMEM((block, LANES), jnp.float32),
            pltpu.VMEM((block, LANES), jnp.float32),
            pltpu.VMEM((rows, 2 * units), jnp.float32),
        ],
        compiler_params=pltpu.CompilerParams(vmem_limit_bytes=min(60 << 20, (16 << 20) + (rows * 24 << 10))),
        cost_estimate=pl.CostEstimate(
            flops=4 * rows * depth * units, bytes_accessed=4 * depth * units, transcendentals=0
        ),
        name="gate_up_last" if last else "gate_up",
    )(*pieces, weights, *((before, mine) if last else ()))


def solution(mesh):
    rows, cols = mesh.shape["row"], mesh.shape["col"]
    devices = rows * cols
    core, x, y = 1, 2, cols
    upper = [cols * 2 * r for r in range(rows // 2)]
    beside = [4 * r for r in range(cols // 4)]

    def swap(value, flip):
        return lax.ppermute(value, AXES, [(here, here ^ flip(here)) for here in range(devices)])

    def near(stage):
        return lambda here: (x, y)[(stage + here) % 2]

    def far(flips):
        return sorted((f for f in flips if f), reverse=True)

    def gather(held, flips):
        got = {f: swap(held, lambda here, f=f: f) for f in far(flips)}
        return jnp.concatenate([held] + [got[f] for f in flips if f], axis=0)

    def add(first, *rest):
        total = first.astype(jnp.float32)
        for part in rest:
            total = total + part.astype(jnp.float32)
        return total.astype(jnp.bfloat16)

    def scatter(sums, flips):
        size = sums.shape[0] // len(flips)
        part = {f: sums[r * size : (r + 1) * size] for r, f in enumerate(flips)}
        got = [swap(part[f], lambda here, f=f: f) for f in far(flips)]
        return add(part[0], *got)

    def collect(own):
        held = gather(gather(own, upper), beside)
        held = jnp.concatenate([held, swap(held, near(0))], axis=0)
        received = swap(held, near(1))
        other = lambda here: core
        return [held, received, swap(held, other), swap(received, other)]

    def combine(sums):
        mine, others = sums
        mine = add(mine, swap(others, lambda here: core))
        size = mine.shape[0] // 2
        mine = add(mine[:size], swap(mine[size:], near(1)))
        size = size // 2
        mine = add(mine[:size], swap(mine[size:], near(0)))
        return scatter(scatter(mine, beside), upper)

    def on_device(tokens, gate_weights, expert_ids, w_in, w_out):
        width = tokens.shape[1]
        units = w_out.shape[1]
        half = width // 2 // LANES * LANES
        step = next(s for s in (512, 256, LANES) if half % s == 0 and (width - half) % s == 0)
        chosen = expert_ids[:, None, :] == jnp.arange(LANES, dtype=jnp.int32)[None, :, None]
        table = jnp.sum(jnp.where(chosen, gate_weights[:, None, :], 0), axis=2).astype(jnp.bfloat16)
        first = collect(tokens[:, :half])
        second = collect(jnp.concatenate([tokens[:, half:], table], axis=1))

        lanes = units // LANES
        weights = w_in[0].reshape(width, 2, lanes, LANES).transpose(0, 2, 1, 3)
        weights = weights.reshape(width * 2 * lanes, LANES)
        mine = lax.axis_index("col") * EXP_DEV + lax.axis_index("row") // (rows // EXP_DEV)
        total = gate_up(first, weights, units, step, 0)
        hidden = gate_up(second, weights, units, step, half, total, mine.reshape(1))
        size = hidden.shape[0] // 2
        outs = []
        for at, to in ((0, half), (half, width)):
            part = jnp.dot(hidden, w_out[0][:, at:to], preferred_element_type=jnp.float32)
            part = part.astype(jnp.bfloat16)
            outs.append(combine((part[:size], part[size:])))
        return jnp.concatenate(outs, axis=1)

    return jax.shard_map(
        on_device,
        mesh=mesh,
        in_specs=(
            P(AXES, None),
            P(AXES, None),
            P(AXES, None),
            P("col", None, None, "row"),
            P("col", "row", None),
        ),
        out_specs=P(AXES, None),
        check_vma=False,
    )
```

time: 106 us -> 84.5 us (0.80)
  waiting for transfers between devices: 43.7 us -> 30.3 us
  Pallas kernels: 0 us -> 9.94 us
  local copies, waits for them, and re-layouts: 16.3 us -> 6.38 us
  matrix products: 9.6 us -> 2.24 us
  other arithmetic: 7.51 us -> 2.37 us
  starting transfers between devices: 28.4 us -> 32.7 us
    ppermute x20 -> x26, waiting for transfers between devices: 43.7 us -> 30.3 us  [swap(): lax.ppermute(value, AXES, [(here, here ^ flip(here)) for here in range(de...]
    unnamed x5 -> x14, local copies, waits for them, and re-layouts: 15.7 us -> 5.23 us
    pallas_call x0 -> x2, Pallas kernels: none -> 9.94 us  [gate_up(): pl.pallas_call(functools.partial(gate_up_kernel, len(pieces), step, units...]
    dot_general x2, matrix products: 9.6 us -> 2.24 us  [on_device(): jnp.dot(hidden, w_out[0][:, at:to], preferred_element_type=jnp.float32)]
    another operation x10 -> x0, other arithmetic: 5.01 us -> none  [gather(): return jnp.stack([block] + [got[r] for r in range(1, sizes[axis])], axis=at)]
    ppermute x20 -> x26, starting transfers between devices: 28.4 us -> 32.7 us  [swap(): lax.ppermute(value, AXES, [(here, here ^ flip(here)) for here in range(de...]
  transfers between devices with their start and end apart: 20 -> 26, of which waited for: 13 -> 9; matrix products, arithmetic and copies ran while one was open for 18% -> 4% of each run, Pallas kernels for 0% -> 7%
where the time goes in v2:
time: 84.5 us; the launch traced here: 84.2 us
  starting transfers between devices  32.7 us (39%)
  waiting for transfers between devices  30.3 us (36%)
  Pallas kernels  9.94 us (12%)
  local copies, waits for them, and re-layouts  6.38 us (8%)
  other arithmetic  2.37 us (3%)
  matrix products  2.24 us (3%)
    ppermute x26, starting transfers between devices, swap(): lax.ppermute(value, AXES, [(here, here ^ flip(here)) for here in range(de...  32.7 us
    ppermute x26, waiting for transfers between devices, swap(): lax.ppermute(value, AXES, [(here, here ^ flip(here)) for here in range(de...  30.3 us
    pallas_call x2, Pallas kernels, gate_up(): pl.pallas_call(functools.partial(gate_up_kernel, len(pieces), step, units...  9.94 us
    unnamed x14, local copies, waits for them, and re-layouts  5.23 us
    dot_general x2, matrix products, on_device(): jnp.dot(hidden, w_out[0][:, at:to], preferred_element_type=jnp.float32)  2.24 us
  transfers between devices with their start and end apart: 26, of which 9 were waited for; matrix products, arithmetic and copies ran while one was open for 4% of the time, Pallas kernels for 7%

profile of v2, /device:TPU:0, one launch (start us, length us, event | category | flops | bytes accessed | tf_op | source)
XLA Modules:
  0.0 84.2 jit_solution(12433080814373700551)
XLA Ops:
  0.0 0.9 %fusion.6 = (bf16[8,3584]{1,0:T(8,128)(2,1)S(1)}, bf16[64,3584]{1,0:T(8,128)(2,1)S(1)}, bf16[8,3584]{1,0:T(8,128)(2,1)S(1)}) fusion(bf16[8,7168]{1,0:T(8,128)(2,1)} %param.5), kind=kLoop, calls=%fused_computation.31 | loop fusion | bytes 286720 | tf_op jit(solution)/shard_map/slice | solution.py:155
  0.9 5.1 %collective-permute-start.9 = (bf16[8,3584]{1,0:T(8,128)(2,1)S(1)}, bf16[8,3584]{1,0:T(8,128)(2,1)S(1)}, u32[]{:S(2)}, u32[]{:S(2)}) collective-permute-start(bf16[8,3584]{1,0:T(8,128)(2,1)S(1)} %get-tuple-element.11), channel_id=1, source_target_pairs={{0,24},{1,25},{2,26},{3,27},{4,28},{5,29},{6,30},{7,31},{8,16},{9,... | collective-permute-start | bytes 172040 | tf_op jit(solution)/shard_map/ppermute | solution.py:108
  6.0 0.0 collective-permute-start.8
  6.0 0.6 collective-permute-start.7
  6.6 0.8 fusion.3
  7.4 2.4 %collective-permute-start.1 = (bf16[8,3712]{1,0:T(8,128)(2,1)S(1)}, bf16[8,3712]{1,0:T(8,128)(2,1)S(1)}, u32[]{:S(2)}, u32[]{:S(2)}) collective-permute-start(bf16[8,3712]{1,0:T(8,128)(2,1)S(1)} %get-tuple-element.14), channel_id=1, source_target_pairs={{0,16},{1,17},{2,18},{3,19},{4,20},{5,21},{6,22},{7,23},{8,24},{9,... | collective-permute-start | bytes 178184 | tf_op jit(solution)/shard_map/ppermute | solution.py:108
  9.8 2.0 %collective-permute-start = (bf16[8,3712]{1,0:T(8,128)(2,1)S(1)}, bf16[8,3712]{1,0:T(8,128)(2,1)S(1)}, u32[]{:S(2)}, u32[]{:S(2)}) collective-permute-start(bf16[8,3712]{1,0:T(8,128)(2,1)S(1)} %get-tuple-element.14), channel_id=1, source_target_pairs={{0,8},{1,9},{2,10},{3,11},{4,12},{5,13},{6,14},{7,15},{8,0},{9,1},... | collective-permute-start | bytes 178184 | tf_op jit(solution)/shard_map/ppermute | solution.py:108
  11.8 0.0 collective-permute-done.9
  11.8 0.8 collective-permute-start.2
  12.6 0.0 collective-permute-done.8
  12.6 0.0 collective-permute-done.7
  12.6 1.6 %collective-permute-start.10 = (bf16[32,3584]{1,0:T(8,128)(2,1)S(1)}, bf16[32,3584]{1,0:T(8,128)(2,1)S(1)}, u32[]{:S(2)}, u32[]{:S(2)}) collective-permute-start(bf16[32,3584]{1,0:T(8,128)(2,1)S(1)} %pad_maximum_fusion.1), channel_id=1, source_target_pairs={{0,2},{1,5},{2,0},{3,7},{4,6},{5,1},{6,4},{7,3},{8,10},{9,13},{10,... | collective-permute-start | bytes 688136 | tf_op jit(solution)/shard_map/ppermute | solution.py:108
  14.2 0.0 collective-permute-done.1
  14.2 0.0 collective-permute-done
  14.2 3.6 %collective-permute-done.2 = bf16[8,3712]{1,0:T(8,128)(2,1)S(1)} collective-permute-done((bf16[8,3712]{1,0:T(8,128)(2,1)S(1)}, bf16[8,3712]{1,0:T(8,128)(2,1)S(1)}, u32[]{:S(2)}, u32[]{:S(2)}) %collective-permute-start.2) | collective-permute-done | bytes 59424 | tf_op jit(solution)/shard_map/ppermute | solution.py:108
  17.8 1.6 %collective-permute-start.3 = (bf16[32,3712]{1,0:T(8,128)(2,1)S(1)}, bf16[32,3712]{1,0:T(8,128)(2,1)S(1)}, u32[]{:S(2)}, u32[]{:S(2)}) collective-permute-start(bf16[32,3712]{1,0:T(8,128)(2,1)S(1)} %pad_maximum_fusion), channel_id=1, source_target_pairs={{0,2},{1,5},{2,0},{3,7},{4,6},{5,1},{6,4},{7,3},{8,10},{9,13},{10,... | collective-permute-start | bytes 712712 | tf_op jit(solution)/shard_map/ppermute | solution.py:108
  19.4 0.0 collective-permute-done.10
  19.5 1.6 %collective-permute-start.11 = (bf16[64,3584]{1,0:T(8,128)(2,1)S(1)}, bf16[64,3584]{1,0:T(8,128)(2,1)S(1)}, u32[]{:S(2)}, u32[]{:S(2)}) collective-permute-start(bf16[64,3584]{1,0:T(8,128)(2,1)S(1)} %constant_dynamic-update-slice_fusion.5.refs_0_), channel_id=1, source_target_pairs={{0,4},{1,3},{2,6},{3,1},{4,0},{5,7},{6,2},{7,5},{8,12},{9,11},{10,... | collective-permute-start | bytes 1376264 | tf_op jit(solution)/shard_map/ppermute | solution.py:108
  21.1 5.5 %collective-permute-done.3 = bf16[32,3712]{1,0:T(8,128)(2,1)S(1)} collective-permute-done((bf16[32,3712]{1,0:T(8,128)(2,1)S(1)}, bf16[32,3712]{1,0:T(8,128)(2,1)S(1)}, u32[]{:S(2)}, u32[]{:S(2)}) %collective-permute-start.3) | collective-permute-done | bytes 237600 | tf_op jit(solution)/shard_map/ppermute | solution.py:108
  26.6 1.6 %collective-permute-start.4 = (bf16[64,3712]{1,0:T(8,128)(2,1)S(1)}, bf16[64,3712]{1,0:T(8,128)(2,1)S(1)}, u32[]{:S(2)}, u32[]{:S(2)}) collective-permute-start(bf16[64,3712]{1,0:T(8,128)(2,1)S(1)} %constant_dynamic-update-slice_fusion.refs_0_), channel_id=1, source_target_pairs={{0,4},{1,3},{2,6},{3,1},{4,0},{5,7},{6,2},{7,5},{8,12},{9,11},{10,... | collective-permute-start | bytes 1425416 | tf_op jit(solution)/shard_map/ppermute | solution.py:108
  28.2 0.0 collective-permute-start.12
  28.2 0.0 collective-permute-done.11.refs_1_
  28.2 0.5 collective-permute-start.13
  28.7 0.0 collective-permute-start.5
  28.7 6.6 %collective-permute-done.4.refs_1_ = bf16[64,3712]{1,0:T(8,128)(2,1)S(1)} collective-permute-done((bf16[64,3712]{1,0:T(8,128)(2,1)S(1)}, bf16[64,3712]{1,0:T(8,128)(2,1)S(1)}, u32[]{:S(2)}, u32[]{:S(2)}) %collective-permute-start.4) | collective-permute-done | bytes 475168 | tf_op jit(solution)/shard_map/ppermute | solution.py:108
  35.3 0.0 collective-permute-start.6
  35.3 0.0 collective-permute-done.12.refs_2_
  35.3 0.0 collective-permute-done.13.refs_3_
  35.3 0.0 copy-start
  35.3 5.2 %copy-done = bf16[1,7168,2,512]{3,2,1,0:T(2,128)(2,1)S(1)} copy-done((bf16[1,7168,2,512]{3,2,1,0:T(2,128)(2,1)S(1)}, bf16[1,7168,2,512]{3,2,1,0:T(2,128)(2,1)}, u32[]{:S(2)}) %copy-start) | copy-done | bytes 14680088
  40.5 5.6 %gate_up.1.refs_5_ = f32[256,1024]{1,0:T(8,128)S(1)} custom-call(bf16[64,3584]{1,0:T(8,128)(2,1)S(1)} %constant_dynamic-update-slice_fusion.5.refs_0_, bf16[64,3584]{1,0:T(8,128)(2,1)S(1)} %collective-permute-done.11.refs_1_, bf16[64,3584]{1,0:T(8,128)(2,1)S(1)} %collective-permute-done.12.refs_2_, bf16[64,3584]{1,0:T(8,128)(2,1)} %collective-permute-done.13.refs_3_, ...), custom_call_target="tpu_custom_call" | custom-call | flops 1879048192 | bytes 7340032 | tf_op jit(solution)/shard_map/gate_up/pallas_call | solution.py:80
  46.1 0.0 collective-permute-done.5.refs_2_
  46.1 0.0 slice-start.1
  46.1 4.4 %gate_up_last.1 = bf16[256,512]{1,0:T(8,128)(2,1)S(1)} custom-call(bf16[64,3712]{1,0:T(8,128)(2,1)S(1)} %constant_dynamic-update-slice_fusion.refs_0_, bf16[64,3712]{1,0:T(8,128)(2,1)S(1)} %collective-permute-done.4.refs_1_, bf16[64,3712]{1,0:T(8,128)(2,1)S(1)} %collective-permute-done.5.refs_2_, bf16[64,3712]{1,0:T(8,128)(2,1)S(1)} %collective-permute-done.6.refs_3_, ...), custom_call_target="tpu_custom_call" | custom-call | flops 1879048192 | bytes 7340032 | tf_op jit(solution)/shard_map/gate_up_last/pallas_call | solution.py:80
  50.5 1.1 %convolution_convert_fusion = bf16[256,3584]{1,0:T(8,128)(2,1)S(1)} fusion(bf16[256,512]{1,0:T(8,128)(2,1)S(1)} %gate_up_last.1, bf16[512,7168]{1,0:T(8,128)(2,1)S(1)} %bitcast.13), kind=kOutput, calls=%fused_computation | convolution fusion | flops 940441600 | bytes 5767168 | tf_op jit(solution)/shard_map/dot_general | solution.py:167
  51.6 0.1 slice.109
  51.7 0.6 collective-permute-start.20
  52.3 1.1 %convolution_convert_fusion.1 = bf16[256,3584]{1,0:T(8,128)(2,1)S(1)} fusion(bf16[256,512]{1,0:T(8,128)(2,1)S(1)} %gate_up_last.1, bf16[512,7168]{1,0:T(8,128)(2,1)S(1)} %bitcast.14), kind=kOutput, calls=%fused_computation.1 | convolution fusion | flops 940441600 | bytes 5767168 | tf_op jit(solution)/shard_map/dot_general | solution.py:167
  53.4 0.1 slice.98
  53.5 0.1 collective-permute-start.14
  53.6 0.8 collective-permute-done.20
  54.4 0.2 add_convert_fusion
  54.6 1.6 %collective-permute-start.21 = (bf16[64,3584]{1,0:T(8,128)(2,1)S(1)}, bf16[64,3584]{1,0:T(8,128)(2,1)S(1)}, u32[]{:S(2)}, u32[]{:S(2)}) collective-permute-start(bf16[64,3584]{1,0:T(8,128)(2,1)S(1)} %slice.111), channel_id=1, source_target_pairs={{0,4},{1,3},{2,6},{3,1},{4,0},{5,7},{6,2},{7,5},{8,12},{9,11},{10,... | collective-permute-start | bytes 1376264 | tf_op jit(solution)/shard_map/ppermute | solution.py:108
  56.2 0.0 collective-permute-done.14
  56.2 0.3 add_convert_fusion.1
  56.6 1.4 %collective-permute-start.15 = (bf16[64,3584]{1,0:T(8,128)(2,1)S(1)}, bf16[64,3584]{1,0:T(8,128)(2,1)S(1)}, u32[]{:S(2)}, u32[]{:S(2)}) collective-permute-start(bf16[64,3584]{1,0:T(8,128)(2,1)S(1)} %slice.100), channel_id=1, source_target_pairs={{0,4},{1,3},{2,6},{3,1},{4,0},{5,7},{6,2},{7,5},{8,12},{9,11},{10,... | collective-permute-start | bytes 1376264 | tf_op jit(solution)/shard_map/ppermute | solution.py:108
  57.9 5.2 %collective-permute-done.21 = bf16[64,3584]{1,0:T(8,128)(2,1)S(1)} collective-permute-done((bf16[64,3584]{1,0:T(8,128)(2,1)S(1)}, bf16[64,3584]{1,0:T(8,128)(2,1)S(1)}, u32[]{:S(2)}, u32[]{:S(2)}) %collective-permute-start.21) | collective-permute-done | bytes 458784 | tf_op jit(solution)/shard_map/ppermute | solution.py:108
  63.2 0.1 add_convert_fusion.2
  63.3 1.6 %collective-permute-start.22 = (bf16[32,3584]{1,0:T(8,128)(2,1)S(1)}, bf16[32,3584]{1,0:T(8,128)(2,1)S(1)}, u32[]{:S(2)}, u32[]{:S(2)}) collective-permute-start(bf16[32,3584]{1,0:T(8,128)(2,1)S(1)} %slice.113), channel_id=1, source_target_pairs={{0,2},{1,5},{2,0},{3,7},{4,6},{5,1},{6,4},{7,3},{8,10},{9,13},{10,... | collective-permute-start | bytes 688136 | tf_op jit(solution)/shard_map/ppermute | solution.py:108
  64.9 5.7 %collective-permute-done.15 = bf16[64,3584]{1,0:T(8,128)(2,1)S(1)} collective-permute-done((bf16[64,3584]{1,0:T(8,128)(2,1)S(1)}, bf16[64,3584]{1,0:T(8,128)(2,1)S(1)}, u32[]{:S(2)}, u32[]{:S(2)}) %collective-permute-start.15) | collective-permute-done | bytes 458784 | tf_op jit(solution)/shard_map/ppermute | solution.py:108
  70.6 0.1 add_convert_fusion.3
  70.7 1.6 %collective-permute-start.16 = (bf16[32,3584]{1,0:T(8,128)(2,1)S(1)}, bf16[32,3584]{1,0:T(8,128)(2,1)S(1)}, u32[]{:S(2)}, u32[]{:S(2)}) collective-permute-start(bf16[32,3584]{1,0:T(8,128)(2,1)S(1)} %slice.102), channel_id=1, source_target_pairs={{0,2},{1,5},{2,0},{3,7},{4,6},{5,1},{6,4},{7,3},{8,10},{9,13},{10,... | collective-permute-start | bytes 688136 | tf_op jit(solution)/shard_map/ppermute | solution.py:108
  72.3 0.0 collective-permute-done.22
  72.3 0.1 add_convert_fusion.4
  72.3 0.9 %collective-permute-start.23 = (bf16[8,3584]{1,0:T(8,128)(2,1)S(1)}, bf16[8,3584]{1,0:T(8,128)(2,1)S(1)}, u32[]{:S(2)}, u32[]{:S(2)}) collective-permute-start(bf16[8,3584]{1,0:T(8,128)(2,1)S(1)} %get-tuple-element.8), channel_id=1, source_target_pairs={{0,24},{1,25},{2,26},{3,27},{4,28},{5,29},{6,30},{7,31},{8,16},{9,... | collective-permute-start | bytes 172040 | tf_op jit(solution)/shard_map/ppermute | solution.py:108
  73.3 3.5 %collective-permute-start.24 = (bf16[8,3584]{1,0:T(8,128)(2,1)S(1)}, bf16[8,3584]{1,0:T(8,128)(2,1)S(1)}, u32[]{:S(2)}, u32[]{:S(2)}) collective-permute-start(bf16[8,3584]{1,0:T(8,128)(2,1)S(1)} %get-tuple-element.10), channel_id=1, source_target_pairs={{0,16},{1,17},{2,18},{3,19},{4,20},{5,21},{6,22},{7,23},{8,24},{9,... | collective-permute-start | bytes 172040 | tf_op jit(solution)/shard_map/ppermute | solution.py:108
  76.8 0.0 collective-permute-done.16
  76.8 0.1 add_convert_fusion.5
  76.9 0.9 %collective-permute-start.17 = (bf16[8,3584]{1,0:T(8,128)(2,1)S(1)}, bf16[8,3584]{1,0:T(8,128)(2,1)S(1)}, u32[]{:S(2)}, u32[]{:S(2)}) collective-permute-start(bf16[8,3584]{1,0:T(8,128)(2,1)S(1)} %get-tuple-element.5), channel_id=1, source_target_pairs={{0,24},{1,25},{2,26},{3,27},{4,28},{5,29},{6,30},{7,31},{8,16},{9,... | collective-permute-start | bytes 172040 | tf_op jit(solution)/shard_map/ppermute | solution.py:108
  77.8 0.7 collective-permute-done.23
  78.5 2.9 %collective-permute-start.18 = (bf16[8,3584]{1,0:T(8,128)(2,1)S(1)}, bf16[8,3584]{1,0:T(8,128)(2,1)S(1)}, u32[]{:S(2)}, u32[]{:S(2)}) collective-permute-start(bf16[8,3584]{1,0:T(8,128)(2,1)S(1)} %get-tuple-element.7), channel_id=1, source_target_pairs={{0,16},{1,17},{2,18},{3,19},{4,20},{5,21},{6,22},{7,23},{8,24},{9,... | collective-permute-start | bytes 172040 | tf_op jit(solution)/shard_map/ppermute | solution.py:108
  81.4 1.5 %collective-permute-done.17 = bf16[8,3584]{1,0:T(8,128)(2,1)S(1)} collective-permute-done((bf16[8,3584]{1,0:T(8,128)(2,1)S(1)}, bf16[8,3584]{1,0:T(8,128)(2,1)S(1)}, u32[]{:S(2)}, u32[]{:S(2)}) %collective-permute-start.17) | collective-permute-done | bytes 57376 | tf_op jit(solution)/shard_map/ppermute | solution.py:108
  82.9 0.6 collective-permute-done.18
  83.6 0.7 pad_maximum_fusion.2
  (31 shorter events, 0.4 us)
Async XLA Ops:
  0.9 11.0 %collective-permute-start.9 = (bf16[8,3584]{1,0:T(8,128)(2,1)S(1)}, bf16[8,3584]{1,0:T(8,128)(2,1)S(1)}, u32[]{:S(2)}, u32[]{:S(2)}) collective-permute-start(bf16[8,3584]{1,0:T(8,128)(2,1)S(1)} %get-tuple-element.11), channel_id=1, source_target_pairs={{0,24},{1,25},{2,26},{3,27},{4,28},{5,29},{6,30},{7,31},{8,16},{9,... | collective-permute-start | bytes 172040 | tf_op jit(solution)/shard_map/ppermute | solution.py:108
  6.0 6.6 %collective-permute-start.8 = (bf16[8,3584]{1,0:T(8,128)(2,1)S(1)}, bf16[8,3584]{1,0:T(8,128)(2,1)S(1)}, u32[]{:S(2)}, u32[]{:S(2)}) collective-permute-start(bf16[8,3584]{1,0:T(8,128)(2,1)S(1)} %get-tuple-element.11), channel_id=1, source_target_pairs={{0,16},{1,17},{2,18},{3,19},{4,20},{5,21},{6,22},{7,23},{8,24},{9,... | collective-permute-start | bytes 172040 | tf_op jit(solution)/shard_map/ppermute | solution.py:108
  6.0 6.6 %collective-permute-start.7 = (bf16[8,3584]{1,0:T(8,128)(2,1)S(1)}, bf16[8,3584]{1,0:T(8,128)(2,1)S(1)}, u32[]{:S(2)}, u32[]{:S(2)}) collective-permute-start(bf16[8,3584]{1,0:T(8,128)(2,1)S(1)} %get-tuple-element.11), channel_id=1, source_target_pairs={{0,8},{1,9},{2,10},{3,11},{4,12},{5,13},{6,14},{7,15},{8,0},{9,1},... | collective-permute-start | bytes 172040 | tf_op jit(solution)/shard_map/ppermute | solution.py:108
  7.4 6.8 %collective-permute-start.1 = (bf16[8,3712]{1,0:T(8,128)(2,1)S(1)}, bf16[8,3712]{1,0:T(8,128)(2,1)S(1)}, u32[]{:S(2)}, u32[]{:S(2)}) collective-permute-start(bf16[8,3712]{1,0:T(8,128)(2,1)S(1)} %get-tuple-element.14), channel_id=1, source_target_pairs={{0,16},{1,17},{2,18},{3,19},{4,20},{5,21},{6,22},{7,23},{8,24},{9,... | collective-permute-start | bytes 178184 | tf_op jit(solution)/shard_map/ppermute | solution.py:108
  9.8 4.4 %collective-permute-start = (bf16[8,3712]{1,0:T(8,128)(2,1)S(1)}, bf16[8,3712]{1,0:T(8,128)(2,1)S(1)}, u32[]{:S(2)}, u32[]{:S(2)}) collective-permute-start(bf16[8,3712]{1,0:T(8,128)(2,1)S(1)} %get-tuple-element.14), channel_id=1, source_target_pairs={{0,8},{1,9},{2,10},{3,11},{4,12},{5,13},{6,14},{7,15},{8,0},{9,1},... | collective-permute-start | bytes 178184 | tf_op jit(solution)/shard_map/ppermute | solution.py:108
  11.8 6.0 %collective-permute-start.2 = (bf16[8,3712]{1,0:T(8,128)(2,1)S(1)}, bf16[8,3712]{1,0:T(8,128)(2,1)S(1)}, u32[]{:S(2)}, u32[]{:S(2)}) collective-permute-start(bf16[8,3712]{1,0:T(8,128)(2,1)S(1)} %get-tuple-element.14), channel_id=1, source_target_pairs={{0,24},{1,25},{2,26},{3,27},{4,28},{5,29},{6,30},{7,31},{8,16},{9,... | collective-permute-start | bytes 178184 | tf_op jit(solution)/shard_map/ppermute | solution.py:108
  12.6 6.8 %collective-permute-start.10 = (bf16[32,3584]{1,0:T(8,128)(2,1)S(1)}, bf16[32,3584]{1,0:T(8,128)(2,1)S(1)}, u32[]{:S(2)}, u32[]{:S(2)}) collective-permute-start(bf16[32,3584]{1,0:T(8,128)(2,1)S(1)} %pad_maximum_fusion.1), channel_id=1, source_target_pairs={{0,2},{1,5},{2,0},{3,7},{4,6},{5,1},{6,4},{7,3},{8,10},{9,13},{10,... | collective-permute-start | bytes 688136 | tf_op jit(solution)/shard_map/ppermute | solution.py:108
  17.8 8.7 %collective-permute-start.3 = (bf16[32,3712]{1,0:T(8,128)(2,1)S(1)}, bf16[32,3712]{1,0:T(8,128)(2,1)S(1)}, u32[]{:S(2)}, u32[]{:S(2)}) collective-permute-start(bf16[32,3712]{1,0:T(8,128)(2,1)S(1)} %pad_maximum_fusion), channel_id=1, source_target_pairs={{0,2},{1,5},{2,0},{3,7},{4,6},{5,1},{6,4},{7,3},{8,10},{9,13},{10,... | collective-permute-start | bytes 712712 | tf_op jit(solution)/shard_map/ppermute | solution.py:108
  19.5 8.7 %collective-permute-start.11 = (bf16[64,3584]{1,0:T(8,128)(2,1)S(1)}, bf16[64,3584]{1,0:T(8,128)(2,1)S(1)}, u32[]{:S(2)}, u32[]{:S(2)}) collective-permute-start(bf16[64,3584]{1,0:T(8,128)(2,1)S(1)} %constant_dynamic-update-slice_fusion.5.refs_0_), channel_id=1, source_target_pairs={{0,4},{1,3},{2,6},{3,1},{4,0},{5,7},{6,2},{7,5},{8,12},{9,11},{10,... | collective-permute-start | bytes 1376264 | tf_op jit(solution)/shard_map/ppermute | solution.py:108
  26.6 8.7 %collective-permute-start.4 = (bf16[64,3712]{1,0:T(8,128)(2,1)S(1)}, bf16[64,3712]{1,0:T(8,128)(2,1)S(1)}, u32[]{:S(2)}, u32[]{:S(2)}) collective-permute-start(bf16[64,3712]{1,0:T(8,128)(2,1)S(1)} %constant_dynamic-update-slice_fusion.refs_0_), channel_id=1, source_target_pairs={{0,4},{1,3},{2,6},{3,1},{4,0},{5,7},{6,2},{7,5},{8,12},{9,11},{10,... | collective-permute-start | bytes 1425416 | tf_op jit(solution)/shard_map/ppermute | solution.py:108
  28.2 7.1 %collective-permute-start.12 = (bf16[64,3584]{1,0:T(8,128)(2,1)S(1)}, bf16[64,3584]{1,0:T(8,128)(2,1)S(1)}, u32[]{:S(2)}, u32[]{:S(2)}) collective-permute-start(bf16[64,3584]{1,0:T(8,128)(2,1)S(1)} %constant_dynamic-update-slice_fusion.5.refs_0_), channel_id=1, source_target_pairs={{0,1},{1,0},{2,3},{3,2},{4,5},{5,4},{6,7},{7,6},{8,9},{9,8},{10,11... | collective-permute-start | bytes 1376264 | tf_op jit(solution)/shard_map/ppermute | solution.py:108
  28.2 7.1 %collective-permute-start.13 = (bf16[64,3584]{1,0:T(8,128)(2,1)S(1)}, bf16[64,3584]{1,0:T(8,128)(2,1)}, u32[]{:S(2)}, u32[]{:S(2)}) collective-permute-start(bf16[64,3584]{1,0:T(8,128)(2,1)S(1)} %collective-permute-done.11.refs_1_), channel_id=1, source_target_pairs={{0,1},{1,0},{2,3},{3,2},{4,5},{5,4},{6,7},{7,6},{8,9},{9,8},{10,11... | collective-permute-start | bytes 1376264 | tf_op jit(solution)/shard_map/ppermute | solution.py:108
  28.7 17.4 %collective-permute-start.5 = (bf16[64,3712]{1,0:T(8,128)(2,1)S(1)}, bf16[64,3712]{1,0:T(8,128)(2,1)S(1)}, u32[]{:S(2)}, u32[]{:S(2)}) collective-permute-start(bf16[64,3712]{1,0:T(8,128)(2,1)S(1)} %constant_dynamic-update-slice_fusion.refs_0_), channel_id=1, source_target_pairs={{0,1},{1,0},{2,3},{3,2},{4,5},{5,4},{6,7},{7,6},{8,9},{9,8},{10,11... | collective-permute-start | bytes 1425416 | tf_op jit(solution)/shard_map/ppermute | solution.py:108
  35.3 10.8 %collective-permute-start.6 = (bf16[64,3712]{1,0:T(8,128)(2,1)S(1)}, bf16[64,3712]{1,0:T(8,128)(2,1)S(1)}, u32[]{:S(2)}, u32[]{:S(2)}) collective-permute-start(bf16[64,3712]{1,0:T(8,128)(2,1)S(1)} %collective-permute-done.4.refs_1_), channel_id=1, source_target_pairs={{0,1},{1,0},{2,3},{3,2},{4,5},{5,4},{6,7},{7,6},{8,9},{9,8},{10,11... | collective-permute-start | bytes 1425416 | tf_op jit(solution)/shard_map/ppermute | solution.py:108
  35.3 5.2 %copy-start = (bf16[1,7168,2,512]{3,2,1,0:T(2,128)(2,1)S(1)}, bf16[1,7168,2,512]{3,2,1,0:T(2,128)(2,1)}, u32[]{:S(2)}) copy-start(bf16[1,7168,2,512]{3,2,1,0:T(2,128)(2,1)} %param.8) | copy-start | bytes 44040196
  40.5 5.6 %copy-start.1 = (bf16[1,7168,2,512]{3,2,1,0:T(2,128)(2,1)S(1)}, bf16[1,7168,2,512]{3,2,1,0:T(2,128)(2,1)}, u32[]{:S(2)}) copy-start(bf16[1,7168,2,512]{3,2,1,0:T(2,128)(2,1)} %param.8) | copy-start | bytes 44040196
  40.5 10.0 %slice-start = ((s8[7340032]{0:T(1024)(128)(4,1)}), s8[3145728]{0:T(1024)(128)(4,1)S(1)}, s32[]{:S(2)}) async-start(s8[7340032]{0:T(1024)(128)(4,1)} %bitcast.11), calls=%async_computation | async-start | bytes 6291456
  46.1 4.4 %slice-start.1 = ((s8[7340032]{0:T(1024)(128)(4,1)}), s8[4194304]{0:T(1024)(128)(4,1)S(1)}, s32[]{:S(2)}) async-start(s8[7340032]{0:T(1024)(128)(4,1)} %bitcast.11), calls=%async_computation.1 | async-start | bytes 8388608
  51.7 2.7 %collective-permute-start.20 = (bf16[128,3584]{1,0:T(8,128)(2,1)S(1)}, bf16[128,3584]{1,0:T(8,128)(2,1)S(1)}, u32[]{:S(2)}, u32[]{:S(2)}) collective-permute-start(bf16[128,3584]{1,0:T(8,128)(2,1)S(1)} %slice.109), channel_id=1, source_target_pairs={{0,1},{1,0},{2,3},{3,2},{4,5},{5,4},{6,7},{7,6},{8,9},{9,8},{10,11... | collective-permute-start | bytes 2752520 | tf_op jit(solution)/shard_map/ppermute | solution.py:108
  53.5 2.8 %collective-permute-start.14 = (bf16[128,3584]{1,0:T(8,128)(2,1)S(1)}, bf16[128,3584]{1,0:T(8,128)(2,1)S(1)}, u32[]{:S(2)}, u32[]{:S(2)}) collective-permute-start(bf16[128,3584]{1,0:T(8,128)(2,1)S(1)} %slice.98), channel_id=1, source_target_pairs={{0,1},{1,0},{2,3},{3,2},{4,5},{5,4},{6,7},{7,6},{8,9},{9,8},{10,11... | collective-permute-start | bytes 2752520 | tf_op jit(solution)/shard_map/ppermute | solution.py:108
  54.6 8.5 %collective-permute-start.21 = (bf16[64,3584]{1,0:T(8,128)(2,1)S(1)}, bf16[64,3584]{1,0:T(8,128)(2,1)S(1)}, u32[]{:S(2)}, u32[]{:S(2)}) collective-permute-start(bf16[64,3584]{1,0:T(8,128)(2,1)S(1)} %slice.111), channel_id=1, source_target_pairs={{0,4},{1,3},{2,6},{3,1},{4,0},{5,7},{6,2},{7,5},{8,12},{9,11},{10,... | collective-permute-start | bytes 1376264 | tf_op jit(solution)/shard_map/ppermute | solution.py:108
  56.6 14.0 %collective-permute-start.15 = (bf16[64,3584]{1,0:T(8,128)(2,1)S(1)}, bf16[64,3584]{1,0:T(8,128)(2,1)S(1)}, u32[]{:S(2)}, u32[]{:S(2)}) collective-permute-start(bf16[64,3584]{1,0:T(8,128)(2,1)S(1)} %slice.100), channel_id=1, source_target_pairs={{0,4},{1,3},{2,6},{3,1},{4,0},{5,7},{6,2},{7,5},{8,12},{9,11},{10,... | collective-permute-start | bytes 1376264 | tf_op jit(solution)/shard_map/ppermute | solution.py:108
  63.3 8.9 %collective-permute-start.22 = (bf16[32,3584]{1,0:T(8,128)(2,1)S(1)}, bf16[32,3584]{1,0:T(8,128)(2,1)S(1)}, u32[]{:S(2)}, u32[]{:S(2)}) collective-permute-start(bf16[32,3584]{1,0:T(8,128)(2,1)S(1)} %slice.113), channel_id=1, source_target_pairs={{0,2},{1,5},{2,0},{3,7},{4,6},{5,1},{6,4},{7,3},{8,10},{9,13},{10,... | collective-permute-start | bytes 688136 | tf_op jit(solution)/shard_map/ppermute | solution.py:108
  70.7 6.1 %collective-permute-start.16 = (bf16[32,3584]{1,0:T(8,128)(2,1)S(1)}, bf16[32,3584]{1,0:T(8,128)(2,1)S(1)}, u32[]{:S(2)}, u32[]{:S(2)}) collective-permute-start(bf16[32,3584]{1,0:T(8,128)(2,1)S(1)} %slice.102), channel_id=1, source_target_pairs={{0,2},{1,5},{2,0},{3,7},{4,6},{5,1},{6,4},{7,3},{8,10},{9,13},{10,... | collective-permute-start | bytes 688136 | tf_op jit(solution)/shard_map/ppermute | solution.py:108
  72.3 6.1 %collective-permute-start.23 = (bf16[8,3584]{1,0:T(8,128)(2,1)S(1)}, bf16[8,3584]{1,0:T(8,128)(2,1)S(1)}, u32[]{:S(2)}, u32[]{:S(2)}) collective-permute-start(bf16[8,3584]{1,0:T(8,128)(2,1)S(1)} %get-tuple-element.8), channel_id=1, source_target_pairs={{0,24},{1,25},{2,26},{3,27},{4,28},{5,29},{6,30},{7,31},{8,16},{9,... | collective-permute-start | bytes 172040 | tf_op jit(solution)/shard_map/ppermute | solution.py:108
  73.3 8.1 %collective-permute-start.25 = (bf16[8,3584]{1,0:T(8,128)(2,1)S(1)}, bf16[8,3584]{1,0:T(8,128)(2,1)S(1)}, u32[]{:S(2)}, u32[]{:S(2)}) collective-permute-start(bf16[8,3584]{1,0:T(8,128)(2,1)S(1)} %get-tuple-element.9), channel_id=1, source_target_pairs={{0,8},{1,9},{2,10},{3,11},{4,12},{5,13},{6,14},{7,15},{8,0},{9,1},... | collective-permute-start | bytes 172040 | tf_op jit(solution)/shard_map/ppermute | solution.py:108
  73.3 8.1 %collective-permute-start.24 = (bf16[8,3584]{1,0:T(8,128)(2,1)S(1)}, bf16[8,3584]{1,0:T(8,128)(2,1)S(1)}, u32[]{:S(2)}, u32[]{:S(2)}) collective-permute-start(bf16[8,3584]{1,0:T(8,128)(2,1)S(1)} %get-tuple-element.10), channel_id=1, source_target_pairs={{0,16},{1,17},{2,18},{3,19},{4,20},{5,21},{6,22},{7,23},{8,24},{9,... | collective-permute-start | bytes 172040 | tf_op jit(solution)/shard_map/ppermute | solution.py:108
  76.9 6.0 %collective-permute-start.17 = (bf16[8,3584]{1,0:T(8,128)(2,1)S(1)}, bf16[8,3584]{1,0:T(8,128)(2,1)S(1)}, u32[]{:S(2)}, u32[]{:S(2)}) collective-permute-start(bf16[8,3584]{1,0:T(8,128)(2,1)S(1)} %get-tuple-element.5), channel_id=1, source_target_pairs={{0,24},{1,25},{2,26},{3,27},{4,28},{5,29},{6,30},{7,31},{8,16},{9,... | collective-permute-start | bytes 172040 | tf_op jit(solution)/shard_map/ppermute | solution.py:108
  77.8 5.1 %collective-permute-start.19 = (bf16[8,3584]{1,0:T(8,128)(2,1)S(1)}, bf16[8,3584]{1,0:T(8,128)(2,1)S(1)}, u32[]{:S(2)}, u32[]{:S(2)}) collective-permute-start(bf16[8,3584]{1,0:T(8,128)(2,1)S(1)} %get-tuple-element.6), channel_id=1, source_target_pairs={{0,8},{1,9},{2,10},{3,11},{4,12},{5,13},{6,14},{7,15},{8,0},{9,1},... | collective-permute-start | bytes 172040 | tf_op jit(solution)/shard_map/ppermute | solution.py:108
  78.5 5.1 %collective-permute-start.18 = (bf16[8,3584]{1,0:T(8,128)(2,1)S(1)}, bf16[8,3584]{1,0:T(8,128)(2,1)S(1)}, u32[]{:S(2)}, u32[]{:S(2)}) collective-permute-start(bf16[8,3584]{1,0:T(8,128)(2,1)S(1)} %get-tuple-element.7), channel_id=1, source_target_pairs={{0,16},{1,17},{2,18},{3,19},{4,20},{5,21},{6,22},{7,23},{8,24},{9,... | collective-permute-start | bytes 172040 | tf_op jit(solution)/shard_map/ppermute | solution.py:108
